TPU v7x, 128 devices: a whole 4x4x4 slice. The times are simulated.
128 devices in a mesh: replica: 8 (over z, core), tp: 16 (over y, x).
Axes of the slice: x: 4, y: 4, z: 4, core: 2. Of those that a mesh axis runs over, the one named last changes fastest.
Arguments:
- hidden: bfloat16 [1024, 8192], P(('replica', 'tp')), may hold values from -64 to 64
- head: bfloat16 [152064, 8192], P(('replica', 'tp'))
- token_ids: int32 [1024], replicated, may hold values from 0 to 152063
Outputs:
- logprob: float32 [1024], P(('replica', 'tp'))
All inputs are finite; a program needn't handle non-finite values.
Results may differ from a plain program's by a relative error of at most 0.0003.
Values may be sent and summed in bfloat16 or wider, within the bound.
A program may use at most 128 MiB of HBM per device.

v0:
```python
import jax
import jax.numpy as jnp
from jax import lax
from jax.sharding import PartitionSpec as P


def in_one_piece(arrays, axis, split_dim, concat_dim, along):
    widths = [a.shape[along] for a in arrays]
    both = jnp.concatenate(arrays, axis=along)
    out = lax.all_to_all(both, axis, split_axis=split_dim, concat_axis=concat_dim, tiled=True)
    return tuple(jnp.split(out, [sum(widths[:k]) for k in range(1, len(widths))], axis=along))


def shards(hidden, head, token_ids):
    device_count = lax.axis_size("replica") * lax.axis_size("tp")
    per_device = hidden.shape[0]
    local_vocab = head.shape[0]
    position = lax.axis_index(("replica", "tp"))
    columns = position * local_vocab + jnp.arange(local_vocab, dtype=jnp.int32)
    gathered = lax.all_gather(hidden, ("replica", "tp"), axis=0, tiled=True)
    logits = lax.dot_general(
        gathered, head, (((1,), (1,)), ((), ())), preferred_element_type=jnp.float32
    )
    row_top = jnp.max(logits, axis=1)
    row_total = jnp.sum(jnp.exp(logits - row_top[:, None]), axis=1)
    row_picked = jnp.sum(jnp.where(columns[None, :] == token_ids[:, None], logits, 0.0), axis=1)
    stats = (row_top, row_total, row_picked)
    row_top, row_total, row_picked = stats
    shaped = (
        row_top.reshape(device_count, per_device),
        row_total.reshape(device_count, per_device),
        row_picked.reshape(device_count, per_device),
    )
    arrived = in_one_piece((shaped[0], shaped[1], shaped[2]), ("replica", "tp"), 0, 0, 1)
    final_top = jnp.max(arrived[0], axis=0)
    final_total = jnp.sum(arrived[1] * jnp.exp(arrived[0] - final_top[None, :]), axis=0)
    final_picked = jnp.sum(arrived[2], axis=0)
    return final_picked - final_top - jnp.log(final_total)


def solution(mesh):
    in_specs = (P(("replica", "tp"), None), P(("replica", "tp"), None), P())
    out_specs = P(("replica", "tp"))
    return jax.shard_map(shards, mesh=mesh, in_specs=in_specs, out_specs=out_specs, check_vma=False)
```

profile of v0, /device:TPU:1, one launch (start us, length us, event | category | flops | bytes accessed | tf_op | source)
XLA Modules:
  0.0 149.2 jit_solution(16097349257414862518)
XLA Ops:
  6.5 0.0 all-gather.2.cloned.1.call-start
  6.5 0.7 all-gather.2.cloned.1.call-update
  7.3 0.0 copy-start
  7.3 86.8 %all-gather.2.cloned.1.call-done = bf16[1024,8192]{1,0:T(8,128)(2,1)} async-done(((bf16[8,8192]{1,0:T(8,128)(2,1)}), bf16[1024,8192]{1,0:T(8,128)(2,1)}) %all-gather.2.cloned.1.call-update) | async-done | bytes 16777232 | tf_op jit(solution)/shard_map/all_gather | solution.py:20
  94.1 27.3 %fusion.1 = (f32[1024]{0:T(1024)S(1)}, f32[1024,1188]{0,1:T(8,128)}) fusion(bf16[1024,8192]{1,0:T(8,128)(2,1)} %all-gather.2.cloned.1.call-done, bf16[1188,8192]{1,0:T(8,128)(2,1)} %param.4), kind=kOutput, calls=%fused_computation.9 | convolution fusion | flops 19932549120 | bytes 41111552 | tf_op jit(solution)/shard_map/dot_general | solution.py:21
  121.4 0.1 reshape.18
  121.5 0.0 copy-done
  121.5 3.1 %exponential_reduce_fusion = (f32[1024]{0:T(1024)S(1)}, f32[1024]{0:T(1024)S(1)}) fusion(f32[1024,1188]{0,1:T(8,128)} %get-tuple-element.10, f32[1024]{0:T(1024)S(1)} %get-tuple-element.9, s32[1024]{0:T(1024)S(1)} %copy-done, s32[1188]{0:T(1024)S(1)} %iota_add_fusion), kind=kLoop, calls=%fused_computation.1 | loop fusion | flops 6080512 | bytes 4887184 | tf_op jit(solution)/shard_map/reduce_sum | solution.py:25
  124.6 0.1 reshape.19
  124.7 0.1 reshape.20
  124.8 0.1 pad_maximum_fusion
  124.9 16.8 %all_to_all.12 = f32[128,1,24]{2,1,0:T(1,128)S(1)} all-to-all(f32[128,1,24]{2,1,0:T(1,128)S(1)} %bitcast.8), channel_id=1, replica_groups=mesh['replica'=8,'tp'=16] {'replica','tp'}, dimensions={0} | all-to-all | bytes 24576 | tf_op jit(solution)/shard_map/all_to_all | solution.py:10
  141.8 0.1 slice_reduce_fusion
  141.9 0.5 log_subtract_fusion
  (2 shorter events, 0.0 us)
Async XLA Ops:
  6.5 87.6 %all-gather.2.cloned.1.call-start = ((), (), s32[]{:S(2)}) async-start(), calls=%async_computation.1 | async-start | bytes 16908288 | tf_op jit(solution)/shard_map/all_gather | solution.py:20
  7.3 114.2 %copy-start = (s32[1024]{0:T(1024)S(1)}, s32[1024]{0:T(1024)}, u32[]{:S(2)}) copy-start(s32[1024]{0:T(1024)} %param.5) | copy-start | bytes 12292
Sparse Core Ops, SparseCore 0:
  10.5 83.5 all-gather.1
where the time goes:
time: 149 us
  waiting for transfers between devices  87.5 us (59%)
  matrix products  27.3 us (18%)
  blocking collectives  16.8 us (11%)
  between operations  13.5 us (9%)
  other arithmetic  3.93 us (3%)
    all_gather x1, waiting for transfers between devices, shards(): gathered = lax.all_gather(hidden, ('replica', 'tp'), axis=0, tiled=True)  86.8 us
    dot_general x1, matrix products, shards(): lax.dot_general(gathered, head, (((1,), (1,)), ((), ())), preferred_eleme...  27.3 us
    all_to_all x1, blocking collectives, in_one_piece(): lax.all_to_all(both, axis, split_axis=split_dim, concat_axis=concat_dim,...  16.8 us
    reduce_sum x1, other arithmetic, shards(): row_total = jnp.sum(jnp.exp(logits - row_top[:, None]), axis=1)  3.15 us
  transfers between devices with their start and end apart: 1, of which 1 were waited for; matrix products, arithmetic and copies ran while one was open for 0% of the time, Pallas kernels for 0%

commit v1 on v0

--- a/solution.py
+++ b/solution.py
@@ -17,7 +17,12 @@
     local_vocab = head.shape[0]
     position = lax.axis_index(("replica", "tp"))
     columns = position * local_vocab + jnp.arange(local_vocab, dtype=jnp.int32)
-    gathered = lax.all_gather(hidden, ("replica", "tp"), axis=0, tiled=True)
+    gathered = jnp.concatenate(
+        lax.all_to_all(
+            jnp.stack([hidden] * lax.axis_size(("replica", "tp"))), ("replica", "tp"), 0, 0
+        ),
+        axis=0,
+    )
     logits = lax.dot_general(
         gathered, head, (((1,), (1,)), ((), ())), preferred_element_type=jnp.float32
     )

time: 149 us -> 319 us (2.14)
  waiting for transfers between devices: 87.5 us -> 227 us
  blocking collectives: 16.8 us -> 42.1 us
  between operations: 13.5 us -> 0.08 us
  starting transfers between devices: 0.01 us -> 11.9 us
  local copies, waits for them, and re-layouts: 0.25 us -> 6.95 us
    all_to_all x0 -> x1, waiting for transfers between devices: none -> 227 us  [shards(): lax.all_to_all(jnp.stack([hidden] * lax.axis_size(('replica', 'tp'))), ('...]
    all_gather x1 -> x0, waiting for transfers between devices: 86.8 us -> none  [shards(): gathered = lax.all_gather(hidden, ('replica', 'tp'), axis=0, tiled=True)]
    all_to_all x1, blocking collectives: 16.8 us -> 42.1 us  [in_one_piece(): lax.all_to_all(both, axis, split_axis=split_dim, concat_axis=concat_dim,...]
    all_to_all x0 -> x1, starting transfers between devices: none -> 11.9 us  [shards(): lax.all_to_all(jnp.stack([hidden] * lax.axis_size(('replica', 'tp'))), ('...]
    another operation x0 -> x1, local copies, waits for them, and re-layouts: none -> 6.71 us  [shards(): jnp.stack([hidden] * lax.axis_size(('replica', 'tp')))]
where the time goes in v1:
time: 319 us
  waiting for transfers between devices  227 us (71%)
  blocking collectives  42.1 us (13%)
  matrix products  27.3 us (9%)
  starting transfers between devices  11.9 us (4%)
  local copies, waits for them, and re-layouts  6.95 us (2%)
  other arithmetic  3.93 us (1%)
    all_to_all x1, waiting for transfers between devices, shards(): lax.all_to_all(jnp.stack([hidden] * lax.axis_size(('replica', 'tp'))), ('...  227 us
    all_to_all x1, blocking collectives, in_one_piece(): lax.all_to_all(both, axis, split_axis=split_dim, concat_axis=concat_dim,...  42.1 us
    dot_general x1, matrix products, shards(): lax.dot_general(gathered, head, (((1,), (1,)), ((), ())), preferred_eleme...  27.3 us
    all_to_all x1, starting transfers between devices, shards(): lax.all_to_all(jnp.stack([hidden] * lax.axis_size(('replica', 'tp'))), ('...  11.9 us
    another operation x1, local copies, waits for them, and re-layouts, shards(): jnp.stack([hidden] * lax.axis_size(('replica', 'tp')))  6.71 us
  transfers between devices with their start and end apart: 1, of which 1 were waited for; matrix products, arithmetic and copies ran while one was open for 0% of the time, Pallas kernels for 0%

profile of v1, /device:TPU:1, one launch (start us, length us, event | category | flops | bytes accessed | tf_op | source)
XLA Modules:
  0.0 319.1 jit_solution(5169966854912995596)
XLA Ops:
  0.0 6.7 %stack.2 = bf16[128,8,8192]{2,1,0:T(8,128)(2,1)} broadcast(bf16[8,8192]{1,0:T(8,128)(2,1)} %param.3), dimensions={1,2} | broadcast | bytes 16908288 | tf_op jit(solution)/shard_map/stack | solution.py:22
  6.7 11.9 %all-to-all-start = ((bf16[128,8,8192]{2,1,0:T(8,128)(2,1)}), bf16[128,8,8192]{2,1,0:T(8,128)(2,1)}, u32[]{:S(2)}, u32[]{:S(2)}) async-start(bf16[128,8,8192]{2,1,0:T(8,128)(2,1)} %stack.2), calls=%async_computation | async-start | bytes 33554432 | tf_op jit(solution)/shard_map/all_to_all | solution.py:21
  18.7 0.0 copy-start
  18.7 226.8 %all-to-all-done = bf16[128,8,8192]{2,1,0:T(8,128)(2,1)} async-done(((bf16[128,8,8192]{2,1,0:T(8,128)(2,1)}), bf16[128,8,8192]{2,1,0:T(8,128)(2,1)}, u32[]{:S(2)}, u32[]{:S(2)}) %all-to-all-start) | async-done | bytes 16777248 | tf_op jit(solution)/shard_map/all_to_all | solution.py:21
  245.5 27.3 %fusion.3 = (f32[1024]{0:T(1024)S(1)}, f32[1024,1188]{0,1:T(8,128)}) fusion(bf16[1188,8192]{1,0:T(8,128)(2,1)} %param.4, bf16[128,8,8192]{2,1,0:T(8,128)(2,1)} %all-to-all-done), kind=kOutput, calls=%fused_computation.11 | convolution fusion | flops 19932549120 | bytes 41111552 | tf_op jit(solution)/shard_map/dot_general | solution.py:26
  272.8 0.1 reshape.24
  272.8 0.0 copy-done
  272.9 3.1 exponential_reduce_fusion
  276.0 0.1 reshape.25
  276.1 0.1 reshape.26
  276.2 0.1 pad_maximum_fusion
  276.3 42.1 %all_to_all.17 = f32[128,1,24]{2,1,0:T(1,128)S(1)} all-to-all(f32[128,1,24]{2,1,0:T(1,128)S(1)} %bitcast.12), channel_id=1, replica_groups=mesh['replica'=8,'tp'=16] {'replica','tp'}, dimensions={0} | all-to-all | bytes 24576 | tf_op jit(solution)/shard_map/all_to_all | solution.py:10
  318.4 0.1 slice_reduce_fusion
  318.5 0.5 log_subtract_fusion
  (2 shorter events, 0.0 us)
Async XLA Ops:
  6.7 238.8 %all-to-all-start = ((bf16[128,8,8192]{2,1,0:T(8,128)(2,1)}), bf16[128,8,8192]{2,1,0:T(8,128)(2,1)}, u32[]{:S(2)}, u32[]{:S(2)}) async-start(bf16[128,8,8192]{2,1,0:T(8,128)(2,1)} %stack.2), calls=%async_computation | async-start | bytes 33554432 | tf_op jit(solution)/shard_map/all_to_all | solution.py:21
  18.7 254.2 %copy-start = (s32[1024]{0:T(1024)S(1)}, s32[1024]{0:T(1024)}, u32[]{:S(2)}) copy-start(s32[1024]{0:T(1024)} %param.5) | copy-start | bytes 12292
